TPU v7x, 128 devices: a whole 4x4x4 slice. The times are simulated.
128 devices in a mesh: img: 16 (over y, z), pix: 8 (over x, core).
Axes of the slice: x: 4, y: 4, z: 4, core: 2. Of those that a mesh axis runs over, the one named last changes fastest.
Arguments:
- images: bfloat16 [6144, 16384], P('img', 'pix'), may hold values from -12 to 12
- inverse_noise_scale: float32 [6144], P('img'), may hold values from 0.4 to 4
- projections: bfloat16 [16384, 16384], P('img', 'pix'), may hold values from -1 to 1
- group_search_blocks: int32 [16, 16], P('img'), may hold values from 0 to 127, as said below
- search_list_count: int32 [16], P('img'), may hold values from 12 to 16, as said below
Outputs:
- projection_sums: float32 [16384, 16384], P('img', 'pix')
- log_evidence: float32 [6144], P(('img', 'pix'))
Inputs may be any that keep to these rules, and one draw needn't show every extreme that they name: `group_search_blocks`: each row lists 16 different block ids; block b is owned by index b // 8 of img. Among the first search_list_count[g] entries of row g no owner appears more than 2 times, and in every draw one owner has 2 of its blocks among the first 2 entries of every row. `search_list_count`: some group's count is 16 in every draw.
All inputs are finite; a program needn't handle non-finite values.
Results may differ from a plain program's by a relative error of at most 0.004.
Values may be sent and summed in bfloat16 or wider, within the bound.
A program may use at most 128 MiB of HBM per device.

v0:
```python
import jax
import jax.numpy as jnp
from jax import lax
from jax.sharding import PartitionSpec as P

BLOCK = 128
CAP = 2
MAXL = 16


def sent_together(arrays, axis, dim, along):
    columns = [a.reshape(*a.shape[:along], -1) for a in arrays]
    both = jnp.concatenate(columns, axis=along)
    filled, at, outs = (lax.all_gather(both, axis, axis=dim, tiled=True), 0, [])
    for a, column in zip(arrays, columns):
        piece = filled[..., at : at + column.shape[along]]
        outs.append(piece.reshape(*piece.shape[:along], *a.shape[along:]))
        at += column.shape[along]
    return tuple(outs)


def normalise(totals, scaling, slot_used):
    logits = totals * scaling[None, :, None, None]
    live_mask = slot_used[:, None, :, None]
    logits = jnp.where(live_mask, logits, jnp.float32(-1e30))
    row_peak = jnp.max(logits, axis=(0, 2, 3), keepdims=True)
    exponent = jnp.where(live_mask, jnp.exp(logits - row_peak), jnp.float32(0.0))
    row_total = jnp.sum(exponent, axis=(0, 2, 3), keepdims=True)
    weights = (exponent / row_total).astype(jnp.bfloat16)
    marginal_likelihood = (row_peak + jnp.log(row_total)).reshape(-1)
    return (weights, marginal_likelihood)


def on_device(images, inverse_noise_scale, projections, group_search_blocks, search_list_count):
    group_rows, pixels = images.shape
    n_groups = lax.axis_size("img")
    n_shares = lax.axis_size("pix")
    owned_blocks = projections.shape[0] // BLOCK
    every_list, every_count = sent_together((group_search_blocks, search_list_count), "img", 0, 1)
    own_index = lax.axis_index("img")
    positions = jnp.arange(MAXL, dtype=jnp.int32)
    slot_ids = jnp.arange(CAP, dtype=jnp.int32)
    live_entry = positions[None, :] < every_count[:, None]
    local_hit = live_entry & (every_list // owned_blocks == own_index)
    slot_rank = jnp.cumsum(local_hit.astype(jnp.int32), axis=1) - 1
    slot_pick = local_hit[:, None, :] & (slot_rank[:, None, :] == slot_ids[None, :, None])
    slot_offset = jnp.sum(jnp.where(slot_pick, every_list[:, None, :] % owned_blocks, 0), axis=2)
    slot_filled = jnp.any(slot_pick, axis=2)
    own_live = positions < search_list_count[0]
    own_owner = group_search_blocks[0] // owned_blocks
    per_owner = jnp.sum(
        (
            own_live[None, :]
            & (own_owner[None, :] == jnp.arange(n_groups, dtype=jnp.int32)[:, None])
        ).astype(jnp.int32),
        axis=1,
    )
    slot_used = slot_ids[None, :] < per_owner[:, None]
    stacked = projections.reshape(owned_blocks, BLOCK, pixels)
    outgoing = jnp.take(stacked, slot_offset.reshape(-1), axis=0).reshape(
        n_groups, CAP, BLOCK, pixels
    )
    everyone = lax.all_gather(images, "img", axis=0, tiled=True).reshape(
        n_groups, group_rows, pixels
    )
    local_scores = jnp.einsum(
        "gcrf,gif->gicr", outgoing, everyone, preferred_element_type=jnp.float32
    )
    partial_value = lax.all_to_all(local_scores, "img", split_axis=0, concat_axis=0, tiled=True)
    share_rows = group_rows // n_shares
    first_row = lax.axis_index("pix") * share_rows
    shares = lax.psum_scatter(partial_value, "pix", scatter_dimension=1, tiled=True)
    scaling = lax.dynamic_slice_in_dim(inverse_noise_scale, first_row, share_rows)
    share_weights, evidence_out = normalise(shares, scaling, slot_used)
    weights = lax.all_gather(share_weights, "pix", axis=1, tiled=True)
    weights_home = lax.all_to_all(weights, "img", split_axis=0, concat_axis=0, tiled=True)
    arriving = jnp.einsum(
        "gicr,gif->gcrf", weights_home, everyone, preferred_element_type=jnp.float32
    ).astype(jnp.bfloat16)
    placement = (
        slot_offset.reshape(-1)[None, :] == jnp.arange(owned_blocks, dtype=jnp.int32)[:, None]
    ) & slot_filled.reshape(-1)[None, :]
    placement_table = placement.astype(jnp.bfloat16)
    running_total = jnp.dot(
        placement_table,
        arriving.reshape(n_groups * CAP, BLOCK * pixels),
        preferred_element_type=jnp.float32,
    )
    return (running_total.reshape(owned_blocks * BLOCK, pixels), evidence_out)


def solution(mesh):
    placed = (P("img", "pix"), P("img"), P("img", "pix"), P("img", None), P("img"))
    return jax.shard_map(
        on_device,
        mesh=mesh,
        in_specs=placed,
        out_specs=(P("img", "pix"), P(("img", "pix"))),
        check_vma=False,
    )
```

profile of v0, /device:TPU:1, one launch (start us, length us, event | category | flops | bytes accessed | tf_op | source)
XLA Modules:
  0.0 452.3 jit_solution(2214554178354910095)
XLA Ops:
  7.2 0.7 all-gather.4.cloned.1.call-update
  8.6 0.7 add_bitcast_fusion
  9.3 18.4 %all-gather = s32[16,1,17]{2,1,0:T(1,128)S(1)} all-gather(s32[1,1,17]{2,1,0:T(1,128)S(1)} %add_bitcast_fusion), channel_id=1, replica_groups=mesh['img'=16,'pix'=8] {'img'}, dimensions={0}, use_global_device_ids=true | all-gather | bytes 1156 | tf_op jit(solution)/shard_map/all_gather | solution.py:14
  27.7 0.2 slice_reduce_fusion
  28.0 0.2 reduce_window_sum.11
  28.6 9.5 %gather_fusion = bf16[32,128,2048]{2,1,0:T(8,128)(2,1)} fusion(bf16[8,128,2048]{2,1,0:T(8,128)(2,1)} %bitcast.28, s32[1024]{0:T(1024)S(1)} %pad_clamp_fusion), kind=kCustom, calls=%fused_computation | custom fusion | bytes 33554560 | tf_op jit(solution)/shard_map/jit(_take)/gather | solution.py:60
  38.1 129.4 %all-gather.4.cloned.1.call-done = bf16[6144,2048]{1,0:T(8,128)(2,1)} async-done(((bf16[384,2048]{1,0:T(8,128)(2,1)}), bf16[6144,2048]{1,0:T(8,128)(2,1)}) %all-gather.4.cloned.1.call-update) | async-done | bytes 25165840 | tf_op jit(solution)/shard_map/all_gather | solution.py:63
  167.5 16.1 %fusion.4 = f32[16,384,2,128]{1,3,2,0:T(8,128)S(1)} fusion(bf16[16,384,2048,1]{2,1,3,0:T(8,128)(2,1)} %bitcast.30, bf16[16,2,128,2048]{3,2,1,0:T(8,128)(2,1)} %bitcast.32, pred[16,2]{1,0:T(8,128)(4,1)S(1)} %copy.13), kind=kOutput, calls=%fused_computation.6 | convolution fusion | flops 6450839552 | bytes 48234528 | tf_op jit(solution)/shard_map/gcrf,gif->gicr/dot_general | solution.py:66
  183.6 77.0 %all_to_all.10 = f32[16,384,2,128]{1,3,2,0:T(8,128)} all-to-all(f32[16,384,2,128]{1,3,2,0:T(8,128)S(1)} %fusion.4), channel_id=1, replica_groups=mesh['img'=16,'pix'=8] {'img'}, dimensions={0} | all-to-all | bytes 12582912 | tf_op jit(solution)/shard_map/all_to_all | solution.py:69
  260.6 6.6 %copy.15 = f32[16,384,2,128]{3,0,2,1:T(8,128)} copy(f32[16,384,2,128]{1,3,2,0:T(8,128)} %all_to_all.10) | data formatting | bytes 12582912 | tf_op jit(solution)/shard_map/all_to_all | solution.py:69
  267.2 0.8 dynamic_slice.3
  268.1 41.6 %reduce-scatter.2.cloned.1.call-done = f32[16,48,2,128]{3,0,2,1:T(8,128)} async-done(((f32[16,384,2,128]{3,0,2,1:T(8,128)}), f32[16,48,2,128]{3,0,2,1:T(8,128)}) %reduce-scatter.2.cloned.1.call-update) | async-done | bytes 786448 | tf_op jit(solution)/shard_map/reduce_scatter | solution.py:72
  309.8 1.9 fusion.7
  311.6 2.0 fusion.8
  313.6 2.3 divide_convert_fusion
  316.0 28.5 %all-gather.6.cloned.1.call-done = bf16[16,384,2,128]{3,0,2,1:T(8,128)(2,1)} async-done(((bf16[16,48,2,128]{3,0,2,1:T(8,128)(2,1)}), bf16[16,384,2,128]{3,0,2,1:T(8,128)(2,1)}) %all-gather.6.cloned.1.call-update) | async-done | bytes 3145744 | tf_op jit(solution)/shard_map/all_gather | solution.py:75
  344.4 4.9 %copy.16 = bf16[16,384,2,128]{1,3,2,0:T(8,128)(2,1)} copy(bf16[16,384,2,128]{3,0,2,1:T(8,128)(2,1)} %all-gather.6.cloned.1.call-done) | data formatting | bytes 6291456 | tf_op jit(solution)/shard_map/all_gather | solution.py:75
  349.4 6.7 %all-to-all-start.1 = ((bf16[16,384,2,128]{1,3,2,0:T(8,128)(2,1)}), bf16[16,384,2,128]{1,3,2,0:T(8,128)(2,1)S(1)}, u32[]{:S(2)}, u32[]{:S(2)}) async-start(bf16[16,384,2,128]{1,3,2,0:T(8,128)(2,1)} %copy.16), calls=%async_computation.2 | async-start | bytes 6291456 | tf_op jit(solution)/shard_map/all_to_all | solution.py:76
  356.5 0.5 log_add_fusion
  357.0 39.8 %all-to-all-done.1 = bf16[16,384,2,128]{1,3,2,0:T(8,128)(2,1)S(1)} async-done(((bf16[16,384,2,128]{1,3,2,0:T(8,128)(2,1)}), bf16[16,384,2,128]{1,3,2,0:T(8,128)(2,1)S(1)}, u32[]{:S(2)}, u32[]{:S(2)}) %all-to-all-start.1) | async-done | bytes 3145760 | tf_op jit(solution)/shard_map/all_to_all | solution.py:76
  396.8 21.2 %convolution_convert_fusion = bf16[16,2,128,2048]{3,2,1,0:T(8,128)(2,1)} fusion(bf16[16,384,2,128]{1,3,2,0:T(8,128)(2,1)S(1)} %all-to-all-done.1, bf16[16,384,2048,1]{2,1,3,0:T(8,128)(2,1)} %bitcast.31), kind=kOutput, calls=%fused_computation.4 | convolution fusion | flops 6450839552 | bytes 45088768 | tf_op jit(solution)/shard_map/gicr,gif->gcrf/dot_general | solution.py:77
  418.0 15.1 %copy.18 = bf16[4,8,128,2048]{3,1,2,0:T(8,128)(2,1)S(1)} copy(bf16[4,8,128,2048]{3,2,1,0:T(8,128)(2,1)} %bitcast.29) | data formatting | bytes 33554432
  433.1 4.4 fusion.17
  437.5 8.3 %reshape.113 = f32[1024,2048]{1,0:T(8,128)} reshape(f32[8,262144]{1,0:T(8,128)} %fusion.17) | data formatting | bytes 16777216 | tf_op jit(solution)/shard_map/reshape | solution.py:89
  (24 shorter events, 1.2 us)
Async XLA Ops:
  7.2 160.3 %all-gather.4.cloned.1.call-start = ((), (), s32[]{:S(2)}) async-start(), calls=%async_computation.3 | async-start | bytes 26738688 | tf_op jit(solution)/shard_map/all_gather | solution.py:63
  7.9 301.9 %reduce-scatter.2.cloned.1.call-start = ((), (), s32[]{:S(2)}) async-start(), calls=%async_computation.4 | async-start | bytes 7077888 | tf_op jit(solution)/shard_map/reduce_scatter | solution.py:72
  183.6 84.4 %copy-start = (s32[1,16]{1,0:T(1,128)S(1)}, s32[1,16]{1,0:T(1,128)}, u32[]{:S(2)}) copy-start(s32[1,16]{1,0:T(1,128)} %param.8) | copy-start | bytes 196
  267.2 77.3 %all-gather.6.cloned.1.call-start = ((), (), s32[]{:S(2)}) async-start(), calls=%async_computation.5 | async-start | bytes 3538944 | tf_op jit(solution)/shard_map/all_gather | solution.py:75
  349.4 47.4 %all-to-all-start.1 = ((bf16[16,384,2,128]{1,3,2,0:T(8,128)(2,1)}), bf16[16,384,2,128]{1,3,2,0:T(8,128)(2,1)S(1)}, u32[]{:S(2)}, u32[]{:S(2)}) async-start(bf16[16,384,2,128]{1,3,2,0:T(8,128)(2,1)} %copy.16), calls=%async_computation.2 | async-start | bytes 6291456 | tf_op jit(solution)/shard_map/all_to_all | solution.py:76
Sparse Core Ops, SparseCore 0:
  10.2 157.2 all-gather.3
  267.3 42.4 reduce-scatter.1
  316.1 28.3 all-gather.5
where the time goes:
time: 456 us; the launch traced here: 452 us
  waiting for transfers between devices  240 us (53%)
  blocking collectives  95.4 us (21%)
  local copies, waits for them, and re-layouts  45.8 us (10%)
  matrix products  41.7 us (9%)
  between operations  14.5 us (3%)
  other arithmetic  8.07 us (2%)
  starting transfers between devices  6.83 us (1%)
    all_gather x1, waiting for transfers between devices, on_device(): lax.all_gather(images, 'img', axis=0, tiled=True)  129 us
    all_to_all x1, blocking collectives, on_device(): lax.all_to_all(local_scores, 'img', split_axis=0, concat_axis=0, tiled=True)  77 us
    reduce_scatter x1, waiting for transfers between devices, on_device(): lax.psum_scatter(partial_value, 'pix', scatter_dimension=1, tiled=True)  41.6 us
    all_to_all x1, waiting for transfers between devices, on_device(): lax.all_to_all(weights, 'img', split_axis=0, concat_axis=0, tiled=True)  39.8 us
    all_gather x1, waiting for transfers between devices, on_device(): weights = lax.all_gather(share_weights, 'pix', axis=1, tiled=True)  28.5 us
    dot_general x1, matrix products, on_device(): jnp.einsum('gicr,gif->gcrf', weights_home, everyone, preferred_element_ty...  21.2 us
    all_gather x1, blocking collectives, sent_together(): filled, at, outs = (lax.all_gather(both, axis, axis=dim, tiled=True), 0, [])  18.4 us
    dot_general x1, matrix products, on_device(): jnp.einsum('gcrf,gif->gicr', outgoing, everyone, preferred_element_type=j...  16.1 us
  transfers between devices with their start and end apart: 4, of which 4 were waited for; matrix products, arithmetic and copies ran while one was open for 3% of the time, Pallas kernels for 0%

commit v1 on v0

v1 whole, which is shorter than its diff:
```python
import jax
import jax.numpy as jnp
from jax import lax
from jax.sharding import PartitionSpec as P

BLOCK = 128
CAP = 2
MAXL = 16


def on_device(images, inverse_noise_scale, projections, group_search_blocks, search_list_count):
    group_rows, pixels = images.shape
    n_groups = lax.axis_size("img")
    n_shares = lax.axis_size("pix")
    share_rows = group_rows // n_shares
    owned_blocks = projections.shape[0] // BLOCK
    own_index = lax.axis_index("img")
    first_row = lax.axis_index("pix") * share_rows
    everyone = lax.all_gather(images, "img", axis=0, tiled=True).reshape(
        n_groups, group_rows, pixels
    )
    small = jnp.concatenate(
        [group_search_blocks.astype(jnp.float32), search_list_count[:, None].astype(jnp.float32),
         lax.dynamic_slice_in_dim(inverse_noise_scale, first_row, share_rows)[None]], axis=1)
    table = lax.all_gather(small, "img", axis=0, tiled=True)
    every_list = table[:, :MAXL].astype(jnp.int32)
    every_count = table[:, MAXL].astype(jnp.int32)
    scaling = table[:, MAXL + 1:]
    positions = jnp.arange(MAXL, dtype=jnp.int32)
    slot_ids = jnp.arange(CAP, dtype=jnp.int32)
    live_entry = positions[None, :] < every_count[:, None]
    local_hit = live_entry & (every_list // owned_blocks == own_index)
    slot_rank = jnp.cumsum(local_hit.astype(jnp.int32), axis=1) - 1
    slot_pick = local_hit[:, None, :] & (slot_rank[:, None, :] == slot_ids[None, :, None])
    slot_offset = jnp.sum(jnp.where(slot_pick, every_list[:, None, :] % owned_blocks, 0), axis=2)
    slot_filled = jnp.any(slot_pick, axis=2)
    stacked = projections.reshape(owned_blocks, BLOCK, pixels)
    outgoing = jnp.take(stacked, slot_offset.reshape(-1), axis=0).reshape(
        n_groups, CAP * BLOCK, pixels
    )
    local_scores = jnp.einsum(
        "gif,gsf->gis", everyone, outgoing, preferred_element_type=jnp.float32
    )
    scores = lax.psum_scatter(local_scores, "pix", scatter_dimension=1, tiled=True)
    live = jnp.repeat(slot_filled, BLOCK, axis=1)[:, None, :]
    logits = jnp.where(live, scores * scaling[:, :, None], jnp.float32(-1e30))
    peak = jnp.max(logits, axis=2)
    total = jnp.sum(jnp.where(live, jnp.exp(logits - peak[:, :, None]), 0.0), axis=2)
    stats = lax.all_gather(jnp.stack([peak, total]), "img", axis=0)
    row_peak = jnp.max(stats[:, 0], axis=0)
    row_total = jnp.sum(stats[:, 1] * jnp.exp(stats[:, 0] - row_peak[None]), axis=0)
    evidence = row_peak + jnp.log(row_total)
    evidence_out = lax.dynamic_index_in_dim(evidence, own_index, 0, keepdims=False)
    exponent = jnp.where(live, jnp.exp(logits - row_peak[:, :, None]), 0.0)
    weights = (exponent / row_total[:, :, None]).astype(jnp.bfloat16)
    weights = lax.all_gather(weights, "pix", axis=1, tiled=True)
    arriving = jnp.einsum(
        "gis,gif->gsf", weights, everyone, preferred_element_type=jnp.float32
    ).astype(jnp.bfloat16)
    placement = (
        slot_offset.reshape(-1)[None, :] == jnp.arange(owned_blocks, dtype=jnp.int32)[:, None]
    ) & slot_filled.reshape(-1)[None, :]
    running_total = jnp.dot(
        placement.astype(jnp.bfloat16),
        arriving.reshape(n_groups * CAP, BLOCK * pixels),
        preferred_element_type=jnp.float32,
    )
    return (running_total.reshape(owned_blocks * BLOCK, pixels), evidence_out)


def solution(mesh):
    placed = (P("img", "pix"), P("img"), P("img", "pix"), P("img", None), P("img"))
    return jax.shard_map(
        on_device,
        mesh=mesh,
        in_specs=placed,
        out_specs=(P("img", "pix"), P(("img", "pix"))),
        check_vma=False,
    )
```

time: 456 us -> 354 us (0.78)
  blocking collectives: 95.4 us -> 37.3 us
  waiting for transfers between devices: 240 us -> 187 us
  other arithmetic: 8.07 us -> 21.5 us
  matrix products: 41.7 us -> 51.9 us
  starting transfers between devices: 6.83 us -> 0.12 us
  local copies, waits for them, and re-layouts: 45.8 us -> 40.6 us
    all_to_all x1 -> x0, blocking collectives: 77 us -> none  [on_device(): lax.all_to_all(local_scores, 'img', split_axis=0, concat_axis=0, tiled=True)]
    all_to_all x1 -> x0, waiting for transfers between devices: 39.8 us -> none  [on_device(): lax.all_to_all(weights, 'img', split_axis=0, concat_axis=0, tiled=True)]
    all_gather x1 -> x2, blocking collectives: 18.4 us -> 37.3 us  [the longest x1 18.9 us: on_device(): stats = lax.all_gather(jnp.stack([peak, total]), 'img', axis=0)]
    unnamed x3 -> x6, local copies, waits for them, and re-layouts: 15.1 us -> 0.03 us
    reshape x0 -> x1, local copies, waits for them, and re-layouts: none -> 14.9 us  [on_device(): arriving.reshape(n_groups * CAP, BLOCK * pixels)]
    all_gather x1, waiting for transfers between devices: 129 us -> 115 us  [on_device(): lax.all_gather(images, 'img', axis=0, tiled=True)]
    select_n x1 -> x2, other arithmetic: 0.01 us -> 14.3 us  [on_device(): jnp.take(stacked, slot_offset.reshape(-1), axis=0)]
    dot_general x3, matrix products: 41.7 us -> 51.9 us  [the longest x1 21.9 us: on_device(): jnp.einsum('gis,gif->gsf', weights, everyone, preferred_element_type=jnp....]
  transfers between devices with their start and end apart: 4 -> 3, of which waited for: 4 -> 3; matrix products, arithmetic and copies ran while one was open for 3% -> 8% of each run, Pallas kernels for 0% -> 0%
where the time goes in v1:
time: 354 us; the launch traced here: 353 us
  waiting for transfers between devices  187 us (53%)
  matrix products  51.9 us (15%)
  local copies, waits for them, and re-layouts  40.6 us (11%)
  blocking collectives  37.3 us (11%)
  other arithmetic  21.5 us (6%)
  between operations  14.5 us (4%)
    all_gather x1, waiting for transfers between devices, on_device(): lax.all_gather(images, 'img', axis=0, tiled=True)  115 us
    reduce_scatter x1, waiting for transfers between devices, on_device(): lax.psum_scatter(local_scores, 'pix', scatter_dimension=1, tiled=True)  41.3 us
    all_gather x1, waiting for transfers between devices, on_device(): weights = lax.all_gather(weights, 'pix', axis=1, tiled=True)  30.4 us
    dot_general x1, matrix products, on_device(): jnp.einsum('gis,gif->gsf', weights, everyone, preferred_element_type=jnp....  21.9 us
    all_gather x1, blocking collectives, on_device(): stats = lax.all_gather(jnp.stack([peak, total]), 'img', axis=0)  18.9 us
    dot_general x1, matrix products, on_device(): jnp.einsum('gif,gsf->gis', everyone, outgoing, preferred_element_type=jnp...  18.7 us
    all_gather x1, blocking collectives, on_device(): table = lax.all_gather(small, 'img', axis=0, tiled=True)  18.4 us
    reshape x1, local copies, waits for them, and re-layouts, on_device(): arriving.reshape(n_groups * CAP, BLOCK * pixels)  14.9 us
  transfers between devices with their start and end apart: 3, of which 3 were waited for; matrix products, arithmetic and copies ran while one was open for 8% of the time, Pallas kernels for 0%

profile of v1, /device:TPU:1, one launch (start us, length us, event | category | flops | bytes accessed | tf_op | source)
XLA Modules:
  0.0 353.3 jit_solution(5376012222658015447)
XLA Ops:
  7.2 0.7 all-gather.5.cloned.1.call-update
  8.6 0.7 convert_element_type.26
  9.4 18.4 %all-gather.1 = f32[16,1,65]{2,1,0:T(1,128)S(1)} all-gather(f32[1,1,65]{2,1,0:T(1,128)S(1)} %maximum_bitcast_fusion), channel_id=1, replica_groups=mesh['img'=16,'pix'=8] {'img'}, dimensions={0}, use_global_device_ids=true | all-gather | bytes 4420 | tf_op jit(solution)/shard_map/all_gather | solution.py:25
  27.8 0.2 fusion.8
  28.1 0.2 reduce_window_sum.11
  28.3 0.1 select_reduce_fusion.1
  28.8 9.5 %gather_fusion = bf16[32,128,2048]{2,1,0:T(8,128)(2,1)} fusion(bf16[8,128,2048]{2,1,0:T(8,128)(2,1)} %bitcast.48, s32[1024]{0:T(1024)S(1)} %pad_clamp_fusion), kind=kCustom, calls=%fused_computation | custom fusion | bytes 33554560 | tf_op jit(solution)/shard_map/jit(_take)/gather | solution.py:38
  38.3 14.3 %bitcast_select_fusion = bf16[16,256,2048]{2,1,0:T(8,128)(2,1)} fusion(pred[16,256]{1,0:T(8,128)(4,1)S(1)} %bitcast.64, bf16[16,256,2048]{2,1,0:T(8,128)(2,1)} %bitcast.47), kind=kLoop, calls=%fused_computation.1 | loop fusion | flops 8388608 | bytes 33558528 | tf_op jit(solution)/shard_map/jit(_take)/select_n | solution.py:38
  52.6 114.9 %all-gather.5.cloned.1.call-done = bf16[6144,2048]{1,0:T(8,128)(2,1)} async-done(((bf16[384,2048]{1,0:T(8,128)(2,1)}), bf16[6144,2048]{1,0:T(8,128)(2,1)}) %all-gather.5.cloned.1.call-update) | async-done | bytes 25165840 | tf_op jit(solution)/shard_map/all_gather | solution.py:19
  167.5 18.7 %convolution_bitcast_fusion = f32[16,384,256]{1,2,0:T(8,128)} fusion(bf16[16,256,2048]{2,1,0:T(8,128)(2,1)} %bitcast_select_fusion, bf16[16,384,2048]{2,1,0:T(8,128)(2,1)} %bitcast.49), kind=kOutput, calls=%fused_computation.4 | convolution fusion | flops 6442450944 | bytes 48234496 | tf_op jit(solution)/shard_map/gif,gsf->gis/dot_general | solution.py:41
  186.2 6.7 %copy.40 = f32[16,384,256]{2,0,1:T(8,128)} copy(f32[16,384,256]{1,2,0:T(8,128)} %convolution_bitcast_fusion) | data formatting | bytes 12582912 | tf_op jit(solution)/shard_map/gif,gsf->gis/dot_general | solution.py:41
  193.0 0.1 fusion.6
  193.2 0.1 copy.36
  193.4 41.3 %reduce-scatter.2.cloned.1.call-done = f32[16,48,256]{2,0,1:T(8,128)} async-done(((f32[16,384,256]{2,0,1:T(8,128)}), f32[16,48,256]{2,0,1:T(8,128)}) %reduce-scatter.2.cloned.1.call-update) | async-done | bytes 786448 | tf_op jit(solution)/shard_map/reduce_scatter | solution.py:44
  234.7 1.4 fusion.1
  236.2 1.5 select_reduce_fusion
  237.8 18.9 %all-gather = f32[32,16,48]{2,1,0:T(8,128)S(1)} all-gather(f32[2,16,48]{2,1,0:T(8,128)S(1)} %pad_maximum_fusion), channel_id=2, replica_groups=mesh['img'=16,'pix'=8] {'img'}, dimensions={0}, use_global_device_ids=true | all-gather | bytes 104448 | tf_op jit(solution)/shard_map/all_gather | solution.py:49
  257.0 2.3 divide_convert_fusion
  259.5 0.5 fusion.19
  260.0 30.4 %all-gather.7.cloned.1.call-done = bf16[16,384,256]{2,0,1:T(8,128)(2,1)} async-done(((bf16[16,48,256]{2,0,1:T(8,128)(2,1)}), bf16[16,384,256]{2,0,1:T(8,128)(2,1)}) %all-gather.7.cloned.1.call-update) | async-done | bytes 3145744 | tf_op jit(solution)/shard_map/all_gather | solution.py:56
  290.4 21.9 %convolution_convert_fusion = bf16[16,256,2048]{2,1,0:T(8,128)(2,1)} fusion(bf16[16,384,2048]{2,1,0:T(8,128)(2,1)} %bitcast.50, bf16[16,384,256]{2,0,1:T(8,128)(2,1)} %all-gather.7.cloned.1.call-done), kind=kOutput, calls=%fused_computation.2 | convolution fusion | flops 6450839552 | bytes 45088768 | tf_op jit(solution)/shard_map/gis,gif->gsf/dot_general | solution.py:57
  312.3 14.9 %reshape.85 = bf16[32,262144]{1,0:T(8,128)(2,1)} reshape(bf16[16,256,2048]{2,1,0:T(8,128)(2,1)} %convolution_convert_fusion) | data formatting | bytes 33554432 | tf_op jit(solution)/shard_map/reshape | solution.py:65
  327.2 11.3 %fusion.14 = f32[8,262144]{1,0:T(8,128)} fusion(bf16[32,262144]{1,0:T(8,128)(2,1)} %reshape.85, s32[32]{0:T(128)S(1)} %eq.41, pred[32]{0:T(512)(128)(4,1)S(1)} %and.47), kind=kOutput, calls=%fused_computation.41 | convolution fusion | flops 134218240 | bytes 25165984 | tf_op jit(solution)/shard_map/dot_general | solution.py:63
  338.5 8.3 %reshape.86 = f32[1024,2048]{1,0:T(8,128)} reshape(f32[8,262144]{1,0:T(8,128)} %fusion.14) | data formatting | bytes 16777216 | tf_op jit(solution)/shard_map/reshape | solution.py:68
  (34 shorter events, 1.6 us)
Async XLA Ops:
  7.2 2.1 copy-start
  7.2 160.3 %all-gather.5.cloned.1.call-start = ((), (), s32[]{:S(2)}) async-start(), calls=%async_computation.1 | async-start | bytes 26738688 | tf_op jit(solution)/shard_map/all_gather | solution.py:19
  7.9 226.8 %reduce-scatter.2.cloned.1.call-start = ((), (), s32[]{:S(2)}) async-start(), calls=%async_computation.2 | async-start | bytes 7077888 | tf_op jit(solution)/shard_map/reduce_scatter | solution.py:44
  192.9 97.5 %all-gather.7.cloned.1.call-start = ((), (), s32[]{:S(2)}) async-start(), calls=%async_computation.3 | async-start | bytes 3538944 | tf_op jit(solution)/shard_map/all_gather | solution.py:56
  312.3 34.5 %copy-start.1 = (f32[384]{0:T(512)S(1)}, f32[384]{0:T(512)}, u32[]{:S(2)}) copy-start(f32[384]{0:T(512)} %param.6) | copy-start | bytes 4612
Sparse Core Ops, SparseCore 0:
  10.2 157.2 all-gather.4
  193.0 41.6 reduce-scatter.1
  259.4 30.9 all-gather.6

commit v2 on v1

v2 whole, which is shorter than its diff:
```python
import functools

import jax
import jax.numpy as jnp
from jax import lax
from jax.experimental import pallas as pl
from jax.experimental.pallas import tpu as pltpu
from jax.sharding import PartitionSpec as P

BLOCK = 128
CAP = 2
MAXL = 16
SIDE = 4
GROUPS = SIDE * SIDE
XS = 4
CHUNKS = 3
ROWS = 128
HALF = ROWS // 2
QUART = HALF // 2
SLOTS = CAP * BLOCK
MESH = pl.DeviceIdType.MESH


def gather_kernel(
    images, projections, ids, scales,
    everyone_out, weights_out, table_out, evidence_out,
    gath, proj, ids_all, scales_all, table, table_s, part, pair_in, x_in, logit, stats, wts, evid,
    ag_send, ag_recv, id_send, id_recv, sc_send, sc_recv, pair_send, pair_recv, x_send, x_recv,
    st_send, st_recv, w_send, w_recv, ev_send, ev_recv, local_sem,
):
    me = lax.axis_index("img")
    pix = lax.axis_index("pix")
    y, z = me // SIDE, lax.rem(me, SIDE)
    x, core = pix // 2, lax.rem(pix, 2)
    partner = 2 * x + 1 - core
    drains = []

    def remote(src, dst, ssem, rsem, device):
        return pltpu.make_async_remote_copy(
            src_ref=src, dst_ref=dst, send_sem=ssem, recv_sem=rsem,
            device_id=device, device_id_type=MESH,
        )

    def send(src, dst, ssem, rsem, device):
        copy = remote(src, dst, ssem, rsem, device)
        copy.start()
        drains.append(copy)

    def arrived(ref, ssem, rsem, device):
        remote(ref, ref, ssem, rsem, device).wait_recv()

    img_peers = [lax.rem(me + k, GROUPS) for k in range(1, GROUPS)]
    pix_peers = [lax.rem(pix + k, 2 * XS) for k in range(1, 2 * XS)]

    loads = []
    for c in range(CHUNKS):
        rows = pl.ds(c * ROWS, ROWS)
        load = pltpu.make_async_copy(images.at[rows, :], gath.at[me, rows, :], local_sem.at[c])
        load.start()
        loads.append(load)
    proj_load = pltpu.make_async_copy(projections, proj, local_sem.at[CHUNKS])
    proj_load.start()
    ids_load = pltpu.make_async_copy(ids, ids_all.at[me], local_sem.at[CHUNKS + 1])
    ids_load.start()
    scales_load = pltpu.make_async_copy(scales, scales_all.at[me], local_sem.at[CHUNKS + 2])
    scales_load.start()

    barrier = pltpu.get_barrier_semaphore()
    for peer in img_peers:
        pl.semaphore_signal(barrier, inc=1, device_id={"img": peer}, device_id_type=MESH)
    for peer in pix_peers:
        pl.semaphore_signal(barrier, inc=1, device_id={"pix": peer}, device_id_type=MESH)
    pl.semaphore_wait(barrier, len(img_peers) + len(pix_peers))

    def group(h, a, b):
        a, b = lax.rem(a + 2 * SIDE, SIDE), lax.rem(b + 2 * SIDE, SIDE)
        return a * SIDE + b if h == 0 else b * SIDE + a

    own = [(y, z), (z, y)]

    def slot(g, c, h, part_of=None):
        first, size = c * ROWS + h * HALF, HALF
        if part_of is not None:
            first, size = first + part_of * QUART, QUART
        return gath.at[g, pl.ds(first, size), :]

    def sems(c, h, k):
        at = (c * 2 + h) * 20 + k
        return ag_send.at[at], ag_recv.at[at]

    STEP = (1, -1)
    ORDER = (0, -1, 1, 2)

    def p1_own(c):
        loads[c].wait()
        for h in range(2):
            a, b = own[h]
            for k in range(2):
                ref = slot(me, c, h)
                send(ref, ref, *sems(c, h, k), {"img": group(h, a + STEP[k], b)})

    def p2_send(c, h, i):
        a, b = own[h]
        for k in range(2):
            ref = slot(group(h, a + ORDER[i], b), c, h)
            send(ref, ref, *sems(c, h, 4 + 2 * i + k), {"img": group(h, a, b + STEP[k])})

    def stage1(c):
        for h in range(2):
            p2_send(c, h, 0)
        for k in range(2):
            for h in range(2):
                a, b = own[h]
                g = group(h, a - STEP[k], b)
                arrived(slot(g, c, h), *sems(c, h, k), {"img": g})
                ref = slot(g, c, h, k)
                send(ref, ref, *sems(c, h, 2 + k), {"img": group(h, a + STEP[k], b)})
                p2_send(c, h, 1 + k)

    def stage2(c):
        for h in range(2):
            a, b = own[h]
            for k in range(2):
                arrived(
                    slot(group(h, a + 2, b), c, h, k), *sems(c, h, 2 + k),
                    {"img": group(h, a - STEP[k], b)},
                )
            p2_send(c, h, 3)

    def stage3(c):
        for i in range(4):
            for h in range(2):
                a, b = own[h]
                for k in range(2):
                    g = group(h, a + ORDER[i], b - STEP[k])
                    source = {"img": group(h, a, b - STEP[k])}
                    arrived(slot(g, c, h), *sems(c, h, 4 + 2 * i + k), source)
                    ref = slot(g, c, h, k)
                    send(ref, ref, *sems(c, h, 12 + 2 * i + k), {"img": group(h, a, b + STEP[k])})

    def stage4(c):
        for i in range(4):
            for h in range(2):
                a, b = own[h]
                for k in range(2):
                    arrived(
                        slot(group(h, a + ORDER[i], b + 2), c, h, k), *sems(c, h, 12 + 2 * i + k),
                        {"img": group(h, a, b - STEP[k])},
                    )

    def exchange_lists():
        ids_load.wait()
        scales_load.wait()
        for k, peer in enumerate(img_peers):
            send(ids_all.at[me], ids_all.at[me], id_send.at[k], id_recv.at[k], {"img": peer})
            send(scales_all.at[me], scales_all.at[me], sc_send.at[k], sc_recv.at[k], {"img": peer})

    def build_table():
        for k in range(GROUPS - 1):
            source = lax.rem(me + GROUPS - 1 - k, GROUPS)
            arrived(ids_all.at[source], id_send.at[k], id_recv.at[k], {"img": source})
            arrived(scales_all.at[source], sc_send.at[k], sc_recv.at[k], {"img": source})
        lists = ids_all[:, 0, :]
        counts = ids_all[:, 1, :]
        lane = lax.broadcasted_iota(jnp.int32, (GROUPS, 128), 1)
        hit = (lane < counts) & ((lists >> 3) == me) & (lane < MAXL)
        first = jnp.min(jnp.where(hit, lane, 128), axis=1, keepdims=True)
        last = jnp.max(jnp.where(hit, lane, -1), axis=1, keepdims=True)
        two = last > first
        offset = lists & 7
        off0 = jnp.sum(jnp.where(lane == first, offset, 0), axis=1, keepdims=True)
        off1 = jnp.sum(jnp.where((lane == last) & two, offset, 0), axis=1, keepdims=True)
        whole = (GROUPS, 128)
        table[0] = jnp.broadcast_to(off0, whole)
        table[1] = jnp.broadcast_to(off1, whole)
        table[2] = jnp.broadcast_to((first < 128).astype(jnp.int32), whole)
        table[3] = jnp.broadcast_to(two.astype(jnp.int32), whole)
        to_smem = pltpu.make_async_copy(table, table_s, local_sem.at[CHUNKS + 3])
        to_smem.start()
        to_smem.wait()
        proj_load.wait()

    def score(c, g):
        rows = gath[g, pl.ds(c * ROWS, ROWS), :]
        for s in range(CAP):
            value = lax.dot_general(
                proj[table_s[s, g, 0]], rows, (((1,), (1,)), ((), ())),
                preferred_element_type=jnp.float32,
            )
            first = pl.multiple_of(lax.rem(g, 2) * SLOTS + s * BLOCK, BLOCK)
            part[c, g // 2, pl.ds(first, BLOCK), :] = value

    def near(v):
        return v + v // 2

    def scores_early(c):
        @pl.loop(0, 9)
        def _(k):
            score(c, group(0, y + near(k // 3), z + near(lax.rem(k, 3))))

    def scores_late(c):
        @pl.loop(0, 4)
        def _(k):
            score(c, group(0, y + 2, z + k))

        @pl.loop(0, 3)
        def _(k):
            score(c, group(0, y + near(k), z + 2))

        for t in range(XS):
            send(part.at[c, 2 * t + 1 - core], pair_in.at[c, t],
                 pair_send.at[c * XS + t], pair_recv.at[c * XS + t], {"pix": partner})

    def post_pair(c):
        for d in (1, 2, 3, 0):
            t = lax.rem(x + d, XS)
            arrived_pair(c, d)
            mine = 2 * t + core
            part[c, mine] = part[c, mine] + pair_in[c, t]
            if d:
                at = c * 3 + d - 1
                send(part.at[c, mine], x_in.at[c, d - 1], x_send.at[at], x_recv.at[at],
                     {"pix": mine})

    def arrived_pair(c, d):
        if d == 1:
            for t in range(XS):
                at = c * XS + t
                arrived(pair_in.at[c, t], pair_send.at[at], pair_recv.at[at], {"pix": partner})

    def filled(g):
        return (table[2, pl.ds(g, 1), :] > 0, table[3, pl.ds(g, 1), :] > 0)

    def post_stats(c):
        for d in (1, 2, 3):
            at = c * 3 + d - 1
            arrived(x_in.at[c, d - 1], x_send.at[at], x_recv.at[at],
                    {"pix": 2 * lax.rem(x + XS - d, XS) + core})
        for j in range(2):
            g = 2 * pix + j
            scaling = scales_all[g, c:c + 1, :]
            live = filled(g)
            peak = jnp.full((1, ROWS), -1e30, jnp.float32)
            for s in range(CAP):
                at = pl.ds(j * SLOTS + s * BLOCK, BLOCK)
                total = (part[c, pix, at, :] + x_in[c, 0, at, :]) + (x_in[c, 1, at, :] + x_in[c, 2, at, :])
                value = jnp.where(live[s], total * scaling, jnp.float32(-1e30))
                logit[at, :] = value
                peak = jnp.maximum(peak, jnp.max(value, axis=0, keepdims=True))
            run = jnp.zeros((1, ROWS), jnp.float32)
            for s in range(CAP):
                value = logit[pl.ds(j * SLOTS + s * BLOCK, BLOCK), :]
                value = jnp.where(live[s], jnp.exp(value - peak), 0.0)
                run = run + jnp.sum(value, axis=0, keepdims=True)
            stats[c, me, j:j + 1, :] = peak
            stats[c, me, 2 + j:3 + j, :] = run
        for k, peer in enumerate(img_peers):
            at = c * (GROUPS - 1) + k
            send(stats.at[c, me], stats.at[c, me], st_send.at[at], st_recv.at[at], {"img": peer})

    def weight_slot(c, p):
        return wts.at[pl.ds(2 * p, 2), :, pl.ds(c * ROWS, ROWS)]

    def post_weights(c):
        for k in range(GROUPS - 1):
            at = c * (GROUPS - 1) + k
            source = lax.rem(me + GROUPS - 1 - k, GROUPS)
            arrived(stats.at[c, source], st_send.at[at], st_recv.at[at], {"img": source})
        for j in range(2):
            g = 2 * pix + j
            live = filled(g)
            peaks = stats[c, :, j, :]
            peak = jnp.max(peaks, axis=0, keepdims=True)
            total = jnp.sum(stats[c, :, 2 + j, :] * jnp.exp(peaks - peak), axis=0, keepdims=True)
            evid[pix, j * CHUNKS + c:j * CHUNKS + c + 1, :] = peak + jnp.log(total)
            inverse = 1.0 / total
            for s in range(CAP):
                value = logit[pl.ds(j * SLOTS + s * BLOCK, BLOCK), :]
                value = jnp.where(live[s], jnp.exp(value - peak) * inverse, 0.0)
                wts[g, pl.ds(s * BLOCK, BLOCK), pl.ds(c * ROWS, ROWS)] = value.astype(jnp.bfloat16)
        mine = weight_slot(c, pix)
        for d in (1, 2, 3):
            at = c * 7 + d
            send(mine, mine, w_send.at[at], w_recv.at[at],
                 {"pix": 2 * lax.rem(x + d, XS) + core})
        send(mine, mine, w_send.at[c * 7], w_recv.at[c * 7], {"pix": partner})

    def post_relay(c):
        for d in (1, 3, 2):
            source = 2 * lax.rem(x + XS - d, XS) + core
            ref = weight_slot(c, source)
            arrived(ref, w_send.at[c * 7 + d], w_recv.at[c * 7 + d], {"pix": source})
            send(ref, ref, w_send.at[c * 7 + 3 + d], w_recv.at[c * 7 + 3 + d], {"pix": partner})

    def post_weights_in(c):
        arrived(weight_slot(c, partner), w_send.at[c * 7], w_recv.at[c * 7], {"pix": partner})
        for d in (1, 3, 2):
            ref = weight_slot(c, 2 * lax.rem(x + XS - d, XS) + 1 - core)
            arrived(ref, w_send.at[c * 7 + 3 + d], w_recv.at[c * 7 + 3 + d], {"pix": partner})

    stores = []

    def store_images(c):
        rows = pl.ds(c * ROWS, ROWS)
        store = pltpu.make_async_copy(
            gath.at[:, rows, :], everyone_out.at[:, rows, :], local_sem.at[CHUNKS + 4 + c]
        )
        store.start()
        stores.append(store)

    p1_own(0)
    exchange_lists()
    stage1(0)
    build_table()
    for c in range(CHUNKS):
        stage2(c)
        if c + 1 < CHUNKS:
            p1_own(c + 1)
        if c:
            post_pair(c - 1)
        stage3(c)
        if c + 1 < CHUNKS:
            stage1(c + 1)
        if c:
            post_stats(c - 1)
        scores_early(c)
        if c:
            post_weights(c - 1)
        stage4(c)
        if c:
            post_relay(c - 1)
        scores_late(c)
        store_images(c)
    last = CHUNKS - 1
    post_pair(last)
    post_stats(last)
    post_weights(last)
    for k, peer in enumerate(pix_peers):
        send(evid.at[pix], evid.at[pix], ev_send.at[k], ev_recv.at[k], {"pix": peer})
    post_relay(last)
    for c in range(CHUNKS):
        post_weights_in(c)
    save_w = pltpu.make_async_copy(wts, weights_out, local_sem.at[2 * CHUNKS + 4])
    save_w.start()
    for k in range(2 * XS - 1):
        source = lax.rem(pix + 2 * XS - 1 - k, 2 * XS)
        arrived(evid.at[source], ev_send.at[k], ev_recv.at[k], {"pix": source})
    evidence_out[...] = evid[me // 2]
    table_out[...] = table[...]
    for copy in drains:
        copy.wait_send()
    for store in stores:
        store.wait()
    save_w.wait()


def gather_and_weigh(images, projections, ids, scales):
    rows, pixels = images.shape
    dma = pltpu.SemaphoreType.DMA
    any_space = pl.BlockSpec(memory_space=pl.ANY)
    vmem = pl.BlockSpec(memory_space=pltpu.VMEM)
    n_img, n_pix = GROUPS - 1, 2 * XS - 1
    return pl.pallas_call(
        gather_kernel,
        out_shape=(
            jax.ShapeDtypeStruct((GROUPS, rows, pixels), jnp.bfloat16),
            jax.ShapeDtypeStruct((GROUPS, SLOTS, rows), jnp.bfloat16),
            jax.ShapeDtypeStruct((4, GROUPS, 128), jnp.int32),
            jax.ShapeDtypeStruct((8, 128), jnp.float32),
        ),
        in_specs=[any_space] * 4,
        out_specs=(any_space, any_space, vmem, vmem),
        scratch_shapes=[
            pltpu.VMEM((GROUPS, rows, pixels), jnp.bfloat16),
            pltpu.VMEM(projections.shape, jnp.bfloat16),
            pltpu.VMEM((GROUPS, 8, 128), jnp.int32),
            pltpu.VMEM((GROUPS, 8, 128), jnp.float32),
            pltpu.VMEM((4, GROUPS, 128), jnp.int32),
            pltpu.SMEM((4, GROUPS, 128), jnp.int32),
            pltpu.VMEM((CHUNKS, 2 * XS, 2 * SLOTS, ROWS), jnp.float32),
            pltpu.VMEM((CHUNKS, XS, 2 * SLOTS, ROWS), jnp.float32),
            pltpu.VMEM((CHUNKS, 3, 2 * SLOTS, ROWS), jnp.float32),
            pltpu.VMEM((2 * SLOTS, ROWS), jnp.float32),
            pltpu.VMEM((CHUNKS, GROUPS, 8, ROWS), jnp.float32),
            pltpu.VMEM((GROUPS, SLOTS, rows), jnp.bfloat16),
            pltpu.VMEM((2 * XS, 8, 128), jnp.float32),
            dma((CHUNKS * 40,)), dma((CHUNKS * 40,)),
            dma((n_img,)), dma((n_img,)),
            dma((n_img,)), dma((n_img,)),
            dma((CHUNKS * XS,)), dma((CHUNKS * XS,)),
            dma((CHUNKS * 3,)), dma((CHUNKS * 3,)),
            dma((CHUNKS * n_img,)), dma((CHUNKS * n_img,)),
            dma((CHUNKS * 7,)), dma((CHUNKS * 7,)),
            dma((n_pix,)), dma((n_pix,)),
            dma((2 * CHUNKS + 5,)),
        ],
        compiler_params=pltpu.CompilerParams(
            collective_id=0, has_side_effects=True, vmem_limit_bytes=60 * 1024 * 1024
        ),
        name="gather_and_weigh",
    )(images, projections, ids, scales)


def sum_kernel(table, images, weights, out):
    g = pl.program_id(1)

    @pl.when(g == 0)
    def _():
        out[...] = jnp.zeros_like(out)

    value = jnp.dot(weights[0], images[0], preferred_element_type=jnp.float32)
    for s in range(CAP):
        at = pl.multiple_of(table[s, g, 0] * BLOCK, BLOCK)
        out[pl.ds(at, BLOCK), :] += value[s * BLOCK:(s + 1) * BLOCK]


def sum_images(table, images, weights, owned):
    groups, rows, pixels = images.shape
    tile = pixels // 2
    return pl.pallas_call(
        sum_kernel,
        out_shape=jax.ShapeDtypeStruct((owned, pixels), jnp.float32),
        grid_spec=pltpu.PrefetchScalarGridSpec(
            num_scalar_prefetch=1,
            grid=(pixels // tile, groups),
            in_specs=[
                pl.BlockSpec((1, rows, tile), lambda f, g, table: (g, 0, f)),
                pl.BlockSpec((1, SLOTS, rows), lambda f, g, table: (g, 0, 0)),
            ],
            out_specs=pl.BlockSpec((owned, tile), lambda f, g, table: (0, f)),
        ),
        compiler_params=pltpu.CompilerParams(
            dimension_semantics=("arbitrary", "arbitrary"), vmem_limit_bytes=48 * 1024 * 1024
        ),
        name="sum_images",
    )(table, images, weights)


def on_device(images, inverse_noise_scale, projections, group_search_blocks, search_list_count):
    group_rows = images.shape[0]
    share_rows = group_rows // lax.axis_size("pix")
    ids = jnp.concatenate([
        jnp.pad(group_search_blocks, ((0, 0), (0, 128 - MAXL))),
        jnp.broadcast_to(search_list_count[:, None], (7, 128)),
    ])
    scales = jnp.pad(inverse_noise_scale.reshape(CHUNKS, ROWS), ((0, 8 - CHUNKS), (0, 0)))
    everyone, weights, table, evidence = gather_and_weigh(
        images, projections.reshape(-1, BLOCK, projections.shape[1]), ids, scales
    )
    sums = sum_images(table, everyone, weights, projections.shape[0])
    odd = lax.rem(lax.axis_index("img"), 2)
    own = lax.dynamic_slice_in_dim(evidence, odd * CHUNKS, CHUNKS, axis=0).reshape(-1)
    first_row = lax.axis_index("pix") * share_rows
    return sums, lax.dynamic_slice_in_dim(own, first_row, share_rows)


def solution(mesh):
    placed = (P("img", "pix"), P("img"), P("img", "pix"), P("img", None), P("img"))
    return jax.shard_map(
        on_device,
        mesh=mesh,
        in_specs=placed,
        out_specs=(P("img", "pix"), P(("img", "pix"))),
        check_vma=False,
    )
```

time: 354 us -> 241 us (0.68)
  Pallas kernels: 0 us -> 233 us
  waiting for transfers between devices: 187 us -> 0 us
  matrix products: 51.9 us -> 0 us
  blocking collectives: 37.3 us -> 0 us
  local copies, waits for them, and re-layouts: 40.6 us -> 5.21 us
  other arithmetic: 21.5 us -> 1.25 us
  between operations: 14.5 us -> 1.3 us
    pallas_call x0 -> x2, Pallas kernels: none -> 233 us  [the longest x1 202 us: gather_and_weigh(): pl.pallas_call(gather_kernel, out_shape=(jax.ShapeDtypeStruct((GROUPS, ro...]
    all_gather x2 -> x0, waiting for transfers between devices: 145 us -> none  [the longest x1 115 us: on_device(): lax.all_gather(images, 'img', axis=0, tiled=True)]
    dot_general x3 -> x0, matrix products: 51.9 us -> none  [the longest x1 21.9 us: on_device(): jnp.einsum('gis,gif->gsf', weights, everyone, preferred_element_type=jnp....]
    reduce_scatter x1 -> x0, waiting for transfers between devices: 41.3 us -> none  [on_device(): lax.psum_scatter(local_scores, 'pix', scatter_dimension=1, tiled=True)]
    all_gather x2 -> x0, blocking collectives: 37.3 us -> none  [the longest x1 18.9 us: on_device(): stats = lax.all_gather(jnp.stack([peak, total]), 'img', axis=0)]
    reshape x3 -> x1, local copies, waits for them, and re-layouts: 23.3 us -> 0.7 us  [on_device(): lax.dynamic_slice_in_dim(evidence, odd * CHUNKS, CHUNKS, axis=0).reshape(-1)]
    select_n x3 -> x0, other arithmetic: 14.3 us -> none  [the longest x2 14.3 us: on_device(): jnp.take(stacked, slot_offset.reshape(-1), axis=0)]
    gather x1 -> x0, local copies, waits for them, and re-layouts: 9.48 us -> none  [on_device(): jnp.take(stacked, slot_offset.reshape(-1), axis=0)]
  transfers between devices with their start and end apart: 3 -> 0, of which waited for: 3 -> 0; matrix products, arithmetic and copies ran while one was open for 8% -> 0% of each run, Pallas kernels for 0% -> 0%
where the time goes in v2:
time: 241 us; the launch traced here: 240 us
  Pallas kernels  233 us (97%)
  local copies, waits for them, and re-layouts  5.21 us (2%)
    pallas_call x1, Pallas kernels, gather_and_weigh(): pl.pallas_call(gather_kernel, out_shape=(jax.ShapeDtypeStruct((GROUPS, ro...  202 us
    pallas_call x1, Pallas kernels, sum_images(): pl.pallas_call(sum_kernel, out_shape=jax.ShapeDtypeStruct((owned, pixels)...  31 us

profile of v2, /device:TPU:1, one launch (start us, length us, event | category | flops | bytes accessed | tf_op | source)
XLA Modules:
  0.0 240.3 jit_solution(16529269797478798436)
XLA Ops:
  1.3 1.3 pad_select_fusion.ids
  2.5 1.3 pad.10.scales
  3.8 201.5 %gather_and_weigh.1 = (bf16[16,384,2048]{2,1,0:T(8,128)(2,1)}, bf16[16,256,384]{2,1,0:T(8,128)(2,1)}, s32[4,16,128]{2,1,0:T(8,128)}, f32[8,128]{1,0:T(8,128)}) custom-call(bf16[384,2048]{1,0:T(8,128)(2,1)} %images.1, bf16[8,128,2048]{2,1,0:T(8,128)(2,1)} %bitcast.6, s32[8,128]{1,0:T(8,128)} %pad_select_fusion.ids, f32[8,128]{1,0:T(8,128)} %pad.10.scales), custom_call_target="tpu_custom_call" | custom-call | tf_op jit(solution)/shard_map/gather_and_weigh/pallas_call | solution.py:363
  205.4 0.7 dynamic-slice_bitcast_fusion
  206.1 0.6 dynamic_slice.7
  206.7 0.0 copy-start
  206.7 1.9 copy-done
  208.5 0.0 copy-start.1
  208.5 0.8 copy-done.1
  209.3 31.0 %sum_images.1 = f32[1024,2048]{1,0:T(8,128)} custom-call(s32[4,16,128]{2,1,0:T(8,128)S(1)} %copy-done.1, bf16[16,384,2048]{2,1,0:T(8,128)(2,1)} %get-tuple-element.7.images, bf16[16,256,384]{2,1,0:T(8,128)(2,1)S(1)} %copy-done), custom_call_target="tpu_custom_call" | custom-call | tf_op jit(solution)/shard_map/sum_images/pallas_call | solution.py:420
Async XLA Ops:
  206.7 1.9 copy-start
  208.5 0.8 copy-start.1

commit v3 on v2

v3 whole, which is shorter than its diff:
```python
import functools

import jax
import jax.numpy as jnp
from jax import lax
from jax.experimental import pallas as pl
from jax.experimental.pallas import tpu as pltpu
from jax.sharding import PartitionSpec as P

BLOCK = 128
CAP = 2
MAXL = 16
SIDE = 4
GROUPS = SIDE * SIDE
XS = 4
FIRST = (0, 128, 256, 320)
SIZE = (128, 128, 64, 64)
CHUNKS = len(SIZE)
WHOLE = 2
ROWS = 128
COLS = 512
SLOTS = CAP * BLOCK
MESH = pl.DeviceIdType.MESH


def gather_kernel(
    images, projections, ids, count, scales,
    late_images, late_weights, early_sums, pairs_out, evidence_out,
    gath, proj, ids_all, scales_all, table, table_s, part_w, part_h, pair_w, pair_h, x_w, x_h,
    logit, stats, wts_w, wts_h, wfull, acc, evid,
    ag_send, ag_recv, id_send, id_recv, sc_send, sc_recv, pair_send, pair_recv, x_send, x_recv,
    st_send, st_recv, w_send, w_recv, ev_send, ev_recv, local_sem,
):
    me = lax.axis_index("img")
    pix = lax.axis_index("pix")
    y, z = me // SIDE, lax.rem(me, SIDE)
    x, core = pix // 2, lax.rem(pix, 2)
    partner = 2 * x + 1 - core
    drains = []
    lane = lax.broadcasted_iota(jnp.int32, (1, 128), 1)
    low = lane < 64

    def remote(src, dst, ssem, rsem, device):
        return pltpu.make_async_remote_copy(
            src_ref=src, dst_ref=dst, send_sem=ssem, recv_sem=rsem,
            device_id=device, device_id_type=MESH,
        )

    def send(src, dst, ssem, rsem, device):
        copy = remote(src, dst, ssem, rsem, device)
        copy.start()
        drains.append(copy)

    def arrived(ref, ssem, rsem, device):
        remote(ref, ref, ssem, rsem, device).wait_recv()

    img_peers = [lax.rem(me + k, GROUPS) for k in range(1, GROUPS)]
    pix_peers = [lax.rem(pix + k, 2 * XS) for k in range(1, 2 * XS)]

    def part(c):
        return part_w.at[c] if c < WHOLE else part_h.at[c - WHOLE]

    def pair_in(c):
        return pair_w.at[c] if c < WHOLE else pair_h.at[c - WHOLE]

    def x_in(c):
        return x_w.at[c] if c < WHOLE else x_h.at[c - WHOLE]

    loads = []
    for c in range(CHUNKS):
        rows = pl.ds(FIRST[c], SIZE[c])
        load = pltpu.make_async_copy(images.at[rows, :], gath.at[me, rows, :], local_sem.at[c])
        load.start()
        loads.append(load)
    proj_load = pltpu.make_async_copy(projections, proj, local_sem.at[CHUNKS])
    proj_load.start()
    ids_all[me, 0:1, 0:MAXL] = ids[...]
    ids_all[me, 1:2, :] = jnp.full((1, 128), count[0], jnp.int32)
    scales_all[me, 0:3, :] = scales[...]

    barrier = pltpu.get_barrier_semaphore()
    for peer in img_peers:
        pl.semaphore_signal(barrier, inc=1, device_id={"img": peer}, device_id_type=MESH)
    for peer in pix_peers:
        pl.semaphore_signal(barrier, inc=1, device_id={"pix": peer}, device_id_type=MESH)
    pl.semaphore_wait(barrier, len(img_peers) + len(pix_peers))

    def group(h, a, b):
        a, b = lax.rem(a + 2 * SIDE, SIDE), lax.rem(b + 2 * SIDE, SIDE)
        return a * SIDE + b if h == 0 else b * SIDE + a

    own = [(y, z), (z, y)]

    def slot(g, c, h, part_of=None):
        size = SIZE[c] // 2
        first = FIRST[c] + h * size
        if part_of is not None:
            size //= 2
            first += part_of * size
        return gath.at[g, pl.ds(first, size), :]

    def sems(c, h, k):
        at = (c * 2 + h) * 20 + k
        return ag_send.at[at], ag_recv.at[at]

    STEP = (1, -1)
    ORDER = (0, -1, 1, 2)

    def p1_own(c):
        loads[c].wait()
        for h in range(2):
            a, b = own[h]
            for k in range(2):
                ref = slot(me, c, h)
                send(ref, ref, *sems(c, h, k), {"img": group(h, a + STEP[k], b)})

    def p2_send(c, h, i):
        a, b = own[h]
        for k in range(2):
            ref = slot(group(h, a + ORDER[i], b), c, h)
            send(ref, ref, *sems(c, h, 4 + 2 * i + k), {"img": group(h, a, b + STEP[k])})

    def stage1(c):
        for h in range(2):
            p2_send(c, h, 0)
        for k in range(2):
            for h in range(2):
                a, b = own[h]
                g = group(h, a - STEP[k], b)
                arrived(slot(g, c, h), *sems(c, h, k), {"img": g})
                ref = slot(g, c, h, k)
                send(ref, ref, *sems(c, h, 2 + k), {"img": group(h, a + STEP[k], b)})
                p2_send(c, h, 1 + k)

    def stage2(c):
        for h in range(2):
            a, b = own[h]
            for k in range(2):
                arrived(
                    slot(group(h, a + 2, b), c, h, k), *sems(c, h, 2 + k),
                    {"img": group(h, a - STEP[k], b)},
                )
            p2_send(c, h, 3)

    def stage3(c, shards):
        for i in shards:
            for h in range(2):
                a, b = own[h]
                for k in range(2):
                    g = group(h, a + ORDER[i], b - STEP[k])
                    source = {"img": group(h, a, b - STEP[k])}
                    arrived(slot(g, c, h), *sems(c, h, 4 + 2 * i + k), source)
                    ref = slot(g, c, h, k)
                    send(ref, ref, *sems(c, h, 12 + 2 * i + k), {"img": group(h, a, b + STEP[k])})

    def stage4(c):
        for i in range(4):
            for h in range(2):
                a, b = own[h]
                for k in range(2):
                    arrived(
                        slot(group(h, a + ORDER[i], b + 2), c, h, k), *sems(c, h, 12 + 2 * i + k),
                        {"img": group(h, a, b - STEP[k])},
                    )

    def exchange_lists():
        for k, peer in enumerate(img_peers):
            send(ids_all.at[me], ids_all.at[me], id_send.at[k], id_recv.at[k], {"img": peer})
            send(scales_all.at[me], scales_all.at[me], sc_send.at[k], sc_recv.at[k], {"img": peer})

    def build_table():
        for k in range(GROUPS - 1):
            source = lax.rem(me + GROUPS - 1 - k, GROUPS)
            arrived(ids_all.at[source], id_send.at[k], id_recv.at[k], {"img": source})
            arrived(scales_all.at[source], sc_send.at[k], sc_recv.at[k], {"img": source})
        lists = ids_all[:, 0, :]
        counts = ids_all[:, 1, :]
        at = lax.broadcasted_iota(jnp.int32, (GROUPS, 128), 1)
        hit = (at < counts) & ((lists >> 3) == me) & (at < MAXL)
        first = jnp.min(jnp.where(hit, at, 128), axis=1, keepdims=True)
        last = jnp.max(jnp.where(hit, at, -1), axis=1, keepdims=True)
        two = last > first
        offset = lists & 7
        off0 = jnp.sum(jnp.where(at == first, offset, 0), axis=1, keepdims=True)
        off1 = jnp.sum(jnp.where((at == last) & two, offset, 0), axis=1, keepdims=True)
        whole = (GROUPS, 128)
        table[0] = jnp.broadcast_to(off0, whole)
        table[1] = jnp.broadcast_to(off1, whole)
        table[2] = jnp.broadcast_to((first < 128).astype(jnp.int32), whole)
        table[3] = jnp.broadcast_to(two.astype(jnp.int32), whole)
        to_smem = pltpu.make_async_copy(table, table_s, local_sem.at[CHUNKS + 1])
        to_smem.start()
        for s in range(CAP):
            for p in range(GROUPS // 2):
                pairs_out[s, p:p + 1, :] = jnp.where(
                    low, table[s, 2 * p:2 * p + 1, :], table[s, 2 * p + 1:2 * p + 2, :])
        to_smem.wait()
        proj_load.wait()

    def against(block, rows):
        return lax.dot_general(
            proj[block], rows, (((1,), (1,)), ((), ())), preferred_element_type=jnp.float32)

    def score(c, g):
        rows = gath[g, pl.ds(FIRST[c], ROWS), :]
        for s in range(CAP):
            first = pl.multiple_of(lax.rem(g, 2) * SLOTS + s * BLOCK, BLOCK)
            part_w[c, g // 2, pl.ds(first, BLOCK), :] = against(table_s[s, g, 0], rows)

    def score_pair(c, t):
        rows = gath[pl.ds(2 * t, 2), pl.ds(FIRST[c], 64), :].reshape(ROWS, gath.shape[2])
        for s in range(CAP):
            one = against(table_s[s, 2 * t, 0], rows)
            other = against(table_s[s, 2 * t + 1, 0], rows)
            part_h[c - WHOLE, t, s * BLOCK:(s + 1) * BLOCK, :] = jnp.where(low, one, other)

    def near(v):
        return v + v // 2

    def row_of(v):
        return lax.rem(y + v, SIDE)

    def scores_early(c):
        if c < WHOLE:
            @pl.loop(0, 9)
            def _(k):
                score(c, group(0, y + near(k // 3), z + near(lax.rem(k, 3))))
        else:
            @pl.loop(0, 3)
            def _(k):
                score_pair(c, 2 * row_of(near(k)) + z // 2)

    def scores_late(c):
        if c < WHOLE:
            @pl.loop(0, 4)
            def _(k):
                score(c, group(0, y + 2, z + k))

            @pl.loop(0, 3)
            def _(k):
                score(c, group(0, y + near(k), z + 2))
        else:
            @pl.loop(0, 3)
            def _(k):
                score_pair(c, 2 * row_of(near(k)) + 1 - z // 2)

            @pl.loop(0, 2)
            def _(k):
                score_pair(c, 2 * row_of(2) + k)

        for t in range(XS):
            send(part(c).at[2 * t + 1 - core], pair_in(c).at[t],
                 pair_send.at[c * XS + t], pair_recv.at[c * XS + t], {"pix": partner})

    def post_pair(c):
        for t in range(XS):
            at = c * XS + t
            arrived(pair_in(c).at[t], pair_send.at[at], pair_recv.at[at], {"pix": partner})
        for d in (2, 1, 3, 0):
            t = lax.rem(x + d, XS)
            mine = 2 * t + core
            part(c)[mine] = part(c)[mine] + pair_in(c)[t]
            if d:
                at = c * 3 + d - 1
                send(part(c).at[mine], x_in(c).at[d - 1], x_send.at[at], x_recv.at[at],
                     {"pix": mine})

    def units(c):
        return range(2 if c < WHOLE else 1)

    def filled(c, j):
        rows = []
        for s in range(CAP):
            one = table[2 + s, pl.ds(2 * pix + j, 1), :]
            if c >= WHOLE:
                one = jnp.where(low, one, table[2 + s, pl.ds(2 * pix + 1, 1), :])
            rows.append(one > 0)
        return rows

    def scaling_of(c, j):
        if c < WHOLE:
            return scales_all[2 * pix + j, c:c + 1, :]
        one = scales_all[2 * pix, 2:3, :]
        other = scales_all[2 * pix + 1, 2:3, :]
        if c == WHOLE:
            return jnp.where(low, one, pltpu.roll(other, 64, 1))
        return jnp.where(low, pltpu.roll(one, 64, 1), other)

    def post_stats(c):
        for d in (1, 2, 3):
            at = c * 3 + d - 1
            arrived(x_in(c).at[d - 1], x_send.at[at], x_recv.at[at],
                    {"pix": 2 * lax.rem(x + XS - d, XS) + core})
        for j in units(c):
            scaling = scaling_of(c, j)
            live = filled(c, j)
            peak = jnp.full((1, ROWS), -1e30, jnp.float32)
            for s in range(CAP):
                at = pl.ds(j * SLOTS + s * BLOCK, BLOCK)
                others = x_in(c)
                total = (part(c)[pix, at, :] + others[0, at, :]) + (others[1, at, :] + others[2, at, :])
                value = jnp.where(live[s], total * scaling, jnp.float32(-1e30))
                logit[c, at, :] = value
                peak = jnp.maximum(peak, jnp.max(value, axis=0, keepdims=True))
            run = jnp.zeros((1, ROWS), jnp.float32)
            for s in range(CAP):
                value = logit[c, pl.ds(j * SLOTS + s * BLOCK, BLOCK), :]
                value = jnp.where(live[s], jnp.exp(value - peak), 0.0)
                run = run + jnp.sum(value, axis=0, keepdims=True)
            stats[c, me, j:j + 1, :] = peak
            stats[c, me, 2 + j:3 + j, :] = run
        for k, peer in enumerate(img_peers):
            at = c * (GROUPS - 1) + k
            send(stats.at[c, me], stats.at[c, me], st_send.at[at], st_recv.at[at], {"img": peer})

    def weight_slot(c, p):
        return wts_w.at[c, pl.ds(2 * p, 2)] if c < WHOLE else wts_h.at[c - WHOLE, p]

    def post_weights(c):
        for k in range(GROUPS - 1):
            at = c * (GROUPS - 1) + k
            source = lax.rem(me + GROUPS - 1 - k, GROUPS)
            arrived(stats.at[c, source], st_send.at[at], st_recv.at[at], {"img": source})
        for j in units(c):
            live = filled(c, j)
            peaks = stats[c, :, j, :]
            peak = jnp.max(peaks, axis=0, keepdims=True)
            total = jnp.sum(stats[c, :, 2 + j, :] * jnp.exp(peaks - peak), axis=0, keepdims=True)
            row = 2 * j + c if c < WHOLE else 2 + c
            evid[pix, row:row + 1, :] = peak + jnp.log(total)
            inverse = 1.0 / total
            for s in range(CAP):
                value = logit[c, pl.ds(j * SLOTS + s * BLOCK, BLOCK), :]
                value = jnp.where(live[s], jnp.exp(value - peak) * inverse, 0.0).astype(jnp.bfloat16)
                if c < WHOLE:
                    wts_w[c, 2 * pix + j, s * BLOCK:(s + 1) * BLOCK, :] = value
                else:
                    wts_h[c - WHOLE, pix, s * BLOCK:(s + 1) * BLOCK, :] = value
        mine = weight_slot(c, pix)
        for d in (2, 1, 3):
            at = c * 7 + d
            send(mine, mine, w_send.at[at], w_recv.at[at],
                 {"pix": 2 * lax.rem(x + d, XS) + core})
        send(mine, mine, w_send.at[c * 7], w_recv.at[c * 7], {"pix": partner})

    def post_relay(c):
        for d in (1, 3, 2):
            source = 2 * lax.rem(x + XS - d, XS) + core
            ref = weight_slot(c, source)
            arrived(ref, w_send.at[c * 7 + d], w_recv.at[c * 7 + d], {"pix": source})
            send(ref, ref, w_send.at[c * 7 + 3 + d], w_recv.at[c * 7 + 3 + d], {"pix": partner})

    def post_weights_in(c):
        arrived(weight_slot(c, partner), w_send.at[c * 7], w_recv.at[c * 7], {"pix": partner})
        for d in (1, 3, 2):
            ref = weight_slot(c, 2 * lax.rem(x + XS - d, XS) + 1 - core)
            arrived(ref, w_send.at[c * 7 + 3 + d], w_recv.at[c * 7 + 3 + d], {"pix": partner})

    def place(c):
        @pl.loop(0, GROUPS)
        def _(g):
            columns = pl.ds(pl.multiple_of(g * ROWS, ROWS), ROWS)
            for b in range(proj.shape[0]):
                value = jnp.zeros((BLOCK, ROWS), jnp.bfloat16)
                for s in range(CAP):
                    value = value + jnp.where(
                        table_s[s, g, 0] == b, wts_w[c, g, s * BLOCK:(s + 1) * BLOCK, :], jnp.bfloat16(0))
                wfull[b * BLOCK:(b + 1) * BLOCK, columns] = value

    def add_images(c, lo, hi):
        @pl.loop(lo, hi)
        def _(u):
            rows = pl.ds(pl.multiple_of(lax.rem(u, 4) * SLOTS, SLOTS), SLOTS)
            columns = pl.ds(pl.multiple_of((u // 4) * COLS, COLS), COLS)
            there = gath[:, pl.ds(FIRST[c], ROWS), columns].reshape(GROUPS * ROWS, COLS)
            value = jnp.dot(wfull[rows, :], there, preferred_element_type=jnp.float32)
            acc[rows, columns] = value if c == 0 else acc[rows, columns] + value

    stores = []

    def store(src, dst):
        copy = pltpu.make_async_copy(src, dst, local_sem.at[CHUNKS + 2 + len(stores)])
        copy.start()
        stores.append(copy)

    def store_images(c):
        store(gath.at[:, pl.ds(FIRST[c], 64), :],
              late_images.at[:, pl.ds(FIRST[c] - FIRST[WHOLE], 64), :])

    p1_own(0)
    exchange_lists()
    stage1(0)
    build_table()

    stage2(0)
    p1_own(1)
    stage3(0, range(4))
    stage1(1)
    scores_early(0)
    stage4(0)
    scores_late(0)

    stage2(1)
    p1_own(2)
    post_pair(0)
    stage3(1, (0, 1))
    post_stats(0)
    stage3(1, (2, 3))
    stage1(2)
    scores_early(1)
    post_weights(0)
    stage4(1)
    scores_late(1)

    stage2(2)
    p1_own(3)
    post_pair(1)
    stage3(2, (0, 1))
    post_relay(0)
    stage3(2, (2, 3))
    post_stats(1)
    stage1(3)
    scores_early(2)
    post_weights_in(0)
    place(0)
    add_images(0, 0, 6)
    stage4(2)
    scores_late(2)
    store_images(2)

    stage2(3)
    post_pair(2)
    post_weights(1)
    stage3(3, range(4))
    post_stats(2)
    add_images(0, 6, 16)
    scores_early(3)
    post_weights(2)
    stage4(3)
    scores_late(3)
    store_images(3)

    post_pair(3)
    post_relay(1)
    post_relay(2)
    post_weights_in(1)
    place(1)
    add_images(1, 0, 8)
    post_stats(3)
    add_images(1, 8, 16)
    store(acc, early_sums)
    post_weights(3)
    for k, peer in enumerate(pix_peers):
        send(evid.at[pix], evid.at[pix], ev_send.at[k], ev_recv.at[k], {"pix": peer})
    post_relay(3)
    post_weights_in(2)
    post_weights_in(3)
    store(wts_h, late_weights)
    for k in range(2 * XS - 1):
        source = lax.rem(pix + 2 * XS - 1 - k, 2 * XS)
        arrived(evid.at[source], ev_send.at[k], ev_recv.at[k], {"pix": source})
    odd = lax.rem(me, 2)
    mine = evid[me // 2]
    for c in range(WHOLE):
        evidence_out[c:c + 1, :] = jnp.where(odd == 0, mine[c:c + 1], mine[2 + c:3 + c])
    third, fourth = mine[4:5], mine[5:6]
    evidence_out[WHOLE:WHOLE + 1, :] = jnp.where(
        odd == 0,
        jnp.where(low, third, pltpu.roll(fourth, 64, 1)),
        jnp.where(low, pltpu.roll(third, 64, 1), fourth),
    )
    for copy in drains:
        copy.wait_send()
    for copy in stores:
        copy.wait()


def gather_and_weigh(images, projections, ids, count, scales):
    rows, pixels = images.shape
    late = rows - FIRST[WHOLE]
    owned = projections.shape[0] * BLOCK
    dma = pltpu.SemaphoreType.DMA
    any_space = pl.BlockSpec(memory_space=pl.ANY)
    vmem = pl.BlockSpec(memory_space=pltpu.VMEM)
    n_img, n_pix = GROUPS - 1, 2 * XS - 1
    f32, bf16 = jnp.float32, jnp.bfloat16
    half = CHUNKS - WHOLE
    return pl.pallas_call(
        gather_kernel,
        out_shape=(
            jax.ShapeDtypeStruct((GROUPS, late, pixels), bf16),
            jax.ShapeDtypeStruct((half, 2 * XS, SLOTS, ROWS), bf16),
            jax.ShapeDtypeStruct((owned, pixels), f32),
            jax.ShapeDtypeStruct((CAP, GROUPS // 2, ROWS), jnp.int32),
            jax.ShapeDtypeStruct((3, 128), f32),
        ),
        in_specs=[any_space, any_space, vmem, pl.BlockSpec(memory_space=pltpu.SMEM), vmem],
        out_specs=(any_space, any_space, any_space, vmem, vmem),
        scratch_shapes=[
            pltpu.VMEM((GROUPS, rows, pixels), bf16),
            pltpu.VMEM(projections.shape, bf16),
            pltpu.VMEM((GROUPS, 8, 128), jnp.int32),
            pltpu.VMEM((GROUPS, 8, 128), f32),
            pltpu.VMEM((4, GROUPS, 128), jnp.int32),
            pltpu.SMEM((4, GROUPS, 128), jnp.int32),
            pltpu.VMEM((WHOLE, 2 * XS, 2 * SLOTS, ROWS), f32),
            pltpu.VMEM((half, 2 * XS, SLOTS, ROWS), f32),
            pltpu.VMEM((WHOLE, XS, 2 * SLOTS, ROWS), f32),
            pltpu.VMEM((half, XS, SLOTS, ROWS), f32),
            pltpu.VMEM((WHOLE, 3, 2 * SLOTS, ROWS), f32),
            pltpu.VMEM((half, 3, SLOTS, ROWS), f32),
            pltpu.VMEM((CHUNKS, 2 * SLOTS, ROWS), f32),
            pltpu.VMEM((CHUNKS, GROUPS, 8, ROWS), f32),
            pltpu.VMEM((WHOLE, GROUPS, SLOTS, ROWS), bf16),
            pltpu.VMEM((half, 2 * XS, SLOTS, ROWS), bf16),
            pltpu.VMEM((owned, GROUPS * ROWS), bf16),
            pltpu.VMEM((owned, pixels), f32),
            pltpu.VMEM((2 * XS, 8, 128), f32),
            dma((CHUNKS * 40,)), dma((CHUNKS * 40,)),
            dma((n_img,)), dma((n_img,)),
            dma((n_img,)), dma((n_img,)),
            dma((CHUNKS * XS,)), dma((CHUNKS * XS,)),
            dma((CHUNKS * 3,)), dma((CHUNKS * 3,)),
            dma((CHUNKS * n_img,)), dma((CHUNKS * n_img,)),
            dma((CHUNKS * 7,)), dma((CHUNKS * 7,)),
            dma((n_pix,)), dma((n_pix,)),
            dma((CHUNKS + 6,)),
        ],
        compiler_params=pltpu.CompilerParams(
            collective_id=0, has_side_effects=True, vmem_limit_bytes=63 * 1024 * 1024
        ),
        name="gather_and_weigh",
    )(images, projections, ids, count, scales)


def sum_kernel(pairs, early, images, weights, out, wfull):
    half = weights.shape[0]
    pair_count = weights.shape[1]
    depth = pair_count * ROWS

    @pl.when(pl.program_id(0) == 0)
    def _():
        for c in range(half):
            for p in range(pair_count):
                at = [pairs[s, p:p + 1, :] for s in range(CAP)]
                value = [weights[c, p, s * BLOCK:(s + 1) * BLOCK, :].astype(jnp.float32) for s in range(CAP)]
                for b in range(wfull.shape[0] // BLOCK):
                    placed = jnp.where(at[0] == b, value[0], 0.0) + jnp.where(at[1] == b, value[1], 0.0)
                    first = (c * pair_count + p) * ROWS
                    wfull[b * BLOCK:(b + 1) * BLOCK, first:first + ROWS] = placed.astype(jnp.bfloat16)

    there = [images[:, c * 64:(c + 1) * 64, :].reshape(depth, images.shape[2]) for c in range(half)]
    for m in range(wfull.shape[0] // SLOTS):
        rows = slice(m * SLOTS, (m + 1) * SLOTS)
        value = early[rows, :]
        for c in range(half):
            value = value + jnp.dot(
                wfull[rows, c * depth:(c + 1) * depth], there[c], preferred_element_type=jnp.float32)
        out[rows, :] = value


def sum_images(pairs, early, images, weights):
    owned, pixels = early.shape
    groups, late, _ = images.shape
    tile = 512
    return pl.pallas_call(
        sum_kernel,
        out_shape=jax.ShapeDtypeStruct((owned, pixels), jnp.float32),
        grid=(pixels // tile,),
        in_specs=[
            pl.BlockSpec(pairs.shape, lambda f: (0, 0, 0)),
            pl.BlockSpec((owned, tile), lambda f: (0, f)),
            pl.BlockSpec((groups, late, tile), lambda f: (0, 0, f)),
            pl.BlockSpec(weights.shape, lambda f: (0, 0, 0, 0)),
        ],
        out_specs=pl.BlockSpec((owned, tile), lambda f: (0, f)),
        scratch_shapes=[pltpu.VMEM((owned, groups * late), jnp.bfloat16)],
        compiler_params=pltpu.CompilerParams(
            dimension_semantics=("arbitrary",), vmem_limit_bytes=48 * 1024 * 1024
        ),
        name="sum_images",
    )(pairs, early, images, weights)


def on_device(images, inverse_noise_scale, projections, group_search_blocks, search_list_count):
    group_rows, pixels = images.shape
    share_rows = group_rows // lax.axis_size("pix")
    late_images, late_weights, early, pairs, evidence = gather_and_weigh(
        images, projections.reshape(-1, BLOCK, pixels), group_search_blocks, search_list_count,
        inverse_noise_scale.reshape(-1, ROWS),
    )
    sums = sum_images(pairs, early, late_images, late_weights)
    first_row = lax.axis_index("pix") * share_rows
    return sums, lax.dynamic_slice_in_dim(evidence.reshape(-1), first_row, share_rows)


def solution(mesh):
    placed = (P("img", "pix"), P("img"), P("img", "pix"), P("img", None), P("img"))
    return jax.shard_map(
        on_device,
        mesh=mesh,
        in_specs=placed,
        out_specs=(P("img", "pix"), P(("img", "pix"))),
        check_vma=False,
    )
```

time: 241 us -> 208 us (0.86)
  Pallas kernels: 233 us -> 203 us
    pallas_call x1, Pallas kernels: 31 us -> 15.1 us  [sum_images(): pl.pallas_call(sum_kernel, out_shape=jax.ShapeDtypeStruct((owned, pixels)...]
    pallas_call x1, Pallas kernels: 202 us -> 188 us  [gather_and_weigh(): pl.pallas_call(gather_kernel, out_shape=(jax.ShapeDtypeStruct((GROUPS, la...]
where the time goes in v3:
time: 208 us
  Pallas kernels  203 us (98%)
  local copies, waits for them, and re-layouts  3.19 us (2%)
    pallas_call x1, Pallas kernels, gather_and_weigh(): pl.pallas_call(gather_kernel, out_shape=(jax.ShapeDtypeStruct((GROUPS, la...  188 us
    pallas_call x1, Pallas kernels, sum_images(): pl.pallas_call(sum_kernel, out_shape=jax.ShapeDtypeStruct((owned, pixels)...  15.1 us

profile of v3, /device:TPU:1, one launch (start us, length us, event | category | flops | bytes accessed | tf_op | source)
XLA Modules:
  0.0 207.7 jit_solution(10106063834466925838)
XLA Ops:
  1.3 188.1 %gather_and_weigh.1 = (bf16[16,128,2048]{2,1,0:T(8,128)(2,1)}, bf16[2,8,256,128]{3,2,1,0:T(8,128)(2,1)}, f32[1024,2048]{1,0:T(8,128)}, s32[2,8,128]{2,1,0:T(8,128)}, f32[3,128]{1,0:T(4,128)}) custom-call(bf16[384,2048]{1,0:T(8,128)(2,1)} %images.1, bf16[8,128,2048]{2,1,0:T(8,128)(2,1)} %bitcast.3, s32[1,16]{1,0:T(1,128)} %ids.1, s32[1]{0:T(128)S(6)} %copy.7.count, ...), custom_call_target="tpu_custom_call" | custom-call | tf_op jit(solution)/shard_map/gather_and_weigh/pallas_call | solution.py:488
  189.4 1.3 dynamic_slice.3
  190.7 0.0 copy-start
  190.7 1.2 copy-done
  191.9 0.0 copy-start.1
  191.9 0.7 copy-done.1
  192.6 15.1 %sum_images.1 = f32[1024,2048]{1,0:T(8,128)} custom-call(s32[2,8,128]{2,1,0:T(8,128)S(1)} %copy-done.1, f32[1024,2048]{1,0:T(8,128)} %get-tuple-element.8.early, bf16[16,128,2048]{2,1,0:T(8,128)(2,1)} %get-tuple-element.9.images, bf16[2,8,256,128]{3,2,1,0:T(8,128)(2,1)S(1)} %copy-done), custom_call_target="tpu_custom_call" | custom-call | tf_op jit(solution)/shard_map/sum_images/pallas_call | solution.py:566
Async XLA Ops:
  190.7 1.2 copy-start
  191.9 0.7 copy-start.1

commit v4 on v3

--- a/solution.py
+++ b/solution.py
@@ -407,47 +407,52 @@
     post_stats(0)
     stage3(1, (2, 3))
     stage1(2)
+    post_weights(0)
     scores_early(1)
-    post_weights(0)
     stage4(1)
+    post_relay(0)
     scores_late(1)
 
     stage2(2)
     p1_own(3)
+    post_weights_in(0)
+    place(0)
     post_pair(1)
-    stage3(2, (0, 1))
-    post_relay(0)
+    stage3(2, (0,))
+    add_images(0, 0, 3)
+    stage3(2, (1,))
+    add_images(0, 3, 6)
     stage3(2, (2, 3))
     post_stats(1)
     stage1(3)
     scores_early(2)
-    post_weights_in(0)
-    place(0)
-    add_images(0, 0, 6)
+    add_images(0, 6, 14)
+    post_weights(1)
     stage4(2)
     scores_late(2)
     store_images(2)
 
     stage2(3)
+    add_images(0, 14, 16)
     post_pair(2)
-    post_weights(1)
-    stage3(3, range(4))
+    stage3(3, (0, 1))
+    post_relay(1)
+    stage3(3, (2, 3))
     post_stats(2)
-    add_images(0, 6, 16)
+    post_weights_in(1)
+    place(1)
     scores_early(3)
     post_weights(2)
     stage4(3)
     scores_late(3)
     store_images(3)
 
+    add_images(1, 0, 4)
     post_pair(3)
-    post_relay(1)
     post_relay(2)
-    post_weights_in(1)
-    place(1)
-    add_images(1, 0, 8)
+    add_images(1, 4, 12)
     post_stats(3)
-    add_images(1, 8, 16)
+    add_images(1, 12, 16)
     store(acc, early_sums)
     post_weights(3)
     for k, peer in enumerate(pix_peers):

time: 208 us -> 203 us (0.976)
  Pallas kernels: 203 us -> 198 us
    pallas_call x1, Pallas kernels: 188 us -> 183 us  [gather_and_weigh(): pl.pallas_call(gather_kernel, out_shape=(jax.ShapeDtypeStruct((GROUPS, la...]
where the time goes in v4:
time: 203 us
  Pallas kernels  198 us (98%)
  local copies, waits for them, and re-layouts  3.19 us (2%)
    pallas_call x1, Pallas kernels, gather_and_weigh(): pl.pallas_call(gather_kernel, out_shape=(jax.ShapeDtypeStruct((GROUPS, la...  183 us
    pallas_call x1, Pallas kernels, sum_images(): pl.pallas_call(sum_kernel, out_shape=jax.ShapeDtypeStruct((owned, pixels)...  15.1 us

profile of v4, /device:TPU:1, one launch (start us, length us, event | category | flops | bytes accessed | tf_op | source)
XLA Modules:
  0.0 202.8 jit_solution(5932635780538377022)
XLA Ops:
  1.3 183.2 %gather_and_weigh.1 = (bf16[16,128,2048]{2,1,0:T(8,128)(2,1)}, bf16[2,8,256,128]{3,2,1,0:T(8,128)(2,1)}, f32[1024,2048]{1,0:T(8,128)}, s32[2,8,128]{2,1,0:T(8,128)}, f32[3,128]{1,0:T(4,128)}) custom-call(bf16[384,2048]{1,0:T(8,128)(2,1)} %images.1, bf16[8,128,2048]{2,1,0:T(8,128)(2,1)} %bitcast.3, s32[1,16]{1,0:T(1,128)} %ids.1, s32[1]{0:T(128)S(6)} %copy.7.count, ...), custom_call_target="tpu_custom_call" | custom-call | tf_op jit(solution)/shard_map/gather_and_weigh/pallas_call | solution.py:493
  184.5 1.3 dynamic_slice.3
  185.8 0.0 copy-start
  185.8 1.2 copy-done
  187.0 0.0 copy-start.1
  187.0 0.7 copy-done.1
  187.7 15.1 %sum_images.1 = f32[1024,2048]{1,0:T(8,128)} custom-call(s32[2,8,128]{2,1,0:T(8,128)S(1)} %copy-done.1, f32[1024,2048]{1,0:T(8,128)} %get-tuple-element.8.early, bf16[16,128,2048]{2,1,0:T(8,128)(2,1)} %get-tuple-element.9.images, bf16[2,8,256,128]{3,2,1,0:T(8,128)(2,1)S(1)} %copy-done), custom_call_target="tpu_custom_call" | custom-call | tf_op jit(solution)/shard_map/sum_images/pallas_call | solution.py:571
Async XLA Ops:
  185.8 1.2 copy-start
  187.0 0.7 copy-start.1

commit v5 on v4

--- a/solution.py
+++ b/solution.py
@@ -415,9 +415,9 @@
 
     stage2(2)
     p1_own(3)
+    post_pair(1)
     post_weights_in(0)
     place(0)
-    post_pair(1)
     stage3(2, (0,))
     add_images(0, 0, 3)
     stage3(2, (1,))

time: 203 us -> 203 us (level)
  no operation moved by 1% of the time
where the time goes in v5:
time: 203 us; the launch traced here: 202 us
  Pallas kernels  198 us (98%)
  local copies, waits for them, and re-layouts  3.19 us (2%)
    pallas_call x1, Pallas kernels, gather_and_weigh(): pl.pallas_call(gather_kernel, out_shape=(jax.ShapeDtypeStruct((GROUPS, la...  183 us
    pallas_call x1, Pallas kernels, sum_images(): pl.pallas_call(sum_kernel, out_shape=jax.ShapeDtypeStruct((owned, pixels)...  15.1 us

profile of v5, /device:TPU:1, one launch (start us, length us, event | category | flops | bytes accessed | tf_op | source)
XLA Modules:
  0.0 202.4 jit_solution(13016385292783915074)
XLA Ops:
  1.3 182.8 %gather_and_weigh.1 = (bf16[16,128,2048]{2,1,0:T(8,128)(2,1)}, bf16[2,8,256,128]{3,2,1,0:T(8,128)(2,1)}, f32[1024,2048]{1,0:T(8,128)}, s32[2,8,128]{2,1,0:T(8,128)}, f32[3,128]{1,0:T(4,128)}) custom-call(bf16[384,2048]{1,0:T(8,128)(2,1)} %images.1, bf16[8,128,2048]{2,1,0:T(8,128)(2,1)} %bitcast.3, s32[1,16]{1,0:T(1,128)} %ids.1, s32[1]{0:T(128)S(6)} %copy.7.count, ...), custom_call_target="tpu_custom_call" | custom-call | tf_op jit(solution)/shard_map/gather_and_weigh/pallas_call | solution.py:493
  184.1 1.3 dynamic_slice.3
  185.4 0.0 copy-start
  185.4 1.2 copy-done
  186.6 0.0 copy-start.1
  186.6 0.7 copy-done.1
  187.3 15.1 %sum_images.1 = f32[1024,2048]{1,0:T(8,128)} custom-call(s32[2,8,128]{2,1,0:T(8,128)S(1)} %copy-done.1, f32[1024,2048]{1,0:T(8,128)} %get-tuple-element.8.early, bf16[16,128,2048]{2,1,0:T(8,128)(2,1)} %get-tuple-element.9.images, bf16[2,8,256,128]{3,2,1,0:T(8,128)(2,1)S(1)} %copy-done), custom_call_target="tpu_custom_call" | custom-call | tf_op jit(solution)/shard_map/sum_images/pallas_call | solution.py:571
Async XLA Ops:
  185.4 1.2 copy-start
  186.6 0.7 copy-start.1
